TPU v7x, 32 devices: a whole 2x2x4 slice. The times are simulated.
32 devices in a mesh: dp: 4 (over z), expert: 8 (over y, x, core).
Axes of the slice: x: 2, y: 2, z: 4, core: 2. Of those that a mesh axis runs over, the one named last changes fastest.
Arguments:
- tokens: bfloat16 [2, 12288, 768], P(None, ('dp', 'expert')), may hold values from -6 to 6
- cotangent: bfloat16 [2, 12288, 768], P(None, ('dp', 'expert')), may hold values from -6 to 6
- token_ids: int32 [2, 12288], P(None, ('dp', 'expert')), may hold values from 0 to 8007, as said below
- hash_table: int32 [8008], replicated, may hold values from 0 to 7, as said below
- segment_ids: int32 [2, 12288], P(None, ('dp', 'expert')), may hold values from 0 to 1, as said below
- query_weight: bfloat16 [768, 768], replicated, may hold values from -0.21875 to 0.21875
- key_weight: bfloat16 [768, 768], replicated, may hold values from -0.21875 to 0.21875
- value_weight: bfloat16 [768, 768], replicated, may hold values from -0.21875 to 0.21875
- output_weight: bfloat16 [768, 768], replicated, may hold values from -2.5 to 2.5
- gain_attn: float32 [768], replicated, may hold values from 0.5 to 1.5
- gain_ffn: float32 [768], replicated, may hold values from 0.5 to 1.5
- expert_in: bfloat16 [8, 768, 3072], P('expert'), may hold values from -0.21875 to 0.21875
- expert_out: bfloat16 [8, 3072, 768], P('expert'), may hold values from -0.109375 to 0.109375
Outputs:
- block_out: bfloat16 [2, 12288, 768], P(None, ('dp', 'expert'))
- grad_tokens: bfloat16 [2, 12288, 768], P(None, ('dp', 'expert'))
- grad_query: float32 [768, 768], replicated
- grad_key: float32 [768, 768], replicated
- grad_value: float32 [768, 768], replicated
- grad_output: float32 [768, 768], replicated
- grad_gain_attn: float32 [768], replicated
- grad_gain_ffn: float32 [768], replicated
- grad_expert_in: float32 [8, 768, 3072], P('expert')
- grad_expert_out: float32 [8, 3072, 768], P('expert')
Inputs may be any that keep to these rules, and one draw needn't show every extreme that they name: hash_table sends 8008 // 8 or more ids to every expert. `token_ids`: in every micro-batch the 384 tokens of one device name any expert, through hash_table, at most 96 times; in every micro-batch one expert is named exactly 96 times by the tokens of every device. `segment_ids`: in each micro-batch a device's block holds either one sequence (all 0) or a sequence of 256 tokens (0) followed by one of the rest (1).
All inputs are finite; a program needn't handle non-finite values.
Results may differ from a plain program's by a relative error of at most 0.012.
Values may be sent and summed in bfloat16 or wider, within the bound.
No kernel may reach another device: no remote copies, remote signals or barrier semaphores. Data moves between devices by JAX's collectives and lax.ppermute only.
A program may use at most 192 MiB of HBM per device.

v0:
```python
import jax
import jax.numpy as jnp
from jax import lax
from jax.sharding import PartitionSpec as P

HEADS = 12
HEAD_DIM = 64
epsilon = 1e-05


def normalize(values, gain):
    return values * lax.rsqrt(jnp.mean(values * values, axis=-1, keepdims=True) + epsilon) * gain


def smooth_slope(values):
    sigmoid_part = jax.nn.sigmoid(values)
    return sigmoid_part * (1.0 + values * (1.0 - sigmoid_part))


def split_heads(matrix, head_count):
    return matrix.reshape(matrix.shape[0], head_count, -1).transpose(1, 0, 2)


def merge_heads(tensor):
    return tensor.transpose(1, 0, 2).reshape(tensor.shape[1], -1)


def masked_scores(query_heads, key_heads, allowed, score_scale):
    scores = (
        jnp.einsum("hqd,hkd->hqk", query_heads, key_heads, preferred_element_type=jnp.float32)
        * score_scale
    )
    return jnp.where(allowed[None], scores, -1e30)


def per_device(
    tokens,
    cotangent,
    token_ids,
    hash_table,
    segment_ids,
    query_weight,
    key_weight,
    value_weight,
    output_weight,
    gain_attn,
    gain_ffn,
    expert_in,
    expert_out,
):
    batches = tokens.shape[0]
    length = tokens.shape[1]
    model_width = tokens.shape[2]
    owners = lax.axis_size("expert")
    capacity = 2 * length // owners
    head_count = HEADS
    score_scale = HEAD_DIM ** (-0.5)
    weight_in = expert_in[0]
    weight_out = expert_out[0]
    position = jnp.arange(length, dtype=jnp.int32)
    float_type = jnp.float32
    half_type = jnp.bfloat16
    dense_total = (
        jnp.zeros(query_weight.shape, float_type),
        jnp.zeros(key_weight.shape, float_type),
        jnp.zeros(value_weight.shape, float_type),
        jnp.zeros(output_weight.shape, float_type),
        jnp.zeros(gain_attn.shape, float_type),
        jnp.zeros(gain_ffn.shape, float_type),
    )
    grad_in_sum = jnp.zeros(weight_in.shape, float_type)
    grad_out_sum = jnp.zeros(weight_out.shape, float_type)
    outputs = []
    grads_in = []
    for batch in range(batches):
        inputs_f = tokens[batch].astype(float_type)
        segments = segment_ids[batch]
        allowed = (position[:, None] >= position[None, :]) & (
            segments[:, None] == segments[None, :]
        )
        normed_attn = normalize(inputs_f, gain_attn).astype(half_type)
        query_heads = split_heads(
            jnp.dot(normed_attn, query_weight, preferred_element_type=float_type).astype(half_type),
            head_count,
        )
        key_heads = split_heads(
            jnp.dot(normed_attn, key_weight, preferred_element_type=float_type).astype(half_type),
            head_count,
        )
        value_heads = split_heads(
            jnp.dot(normed_attn, value_weight, preferred_element_type=float_type).astype(half_type),
            head_count,
        )
        scores = masked_scores(query_heads, key_heads, allowed, score_scale)
        row_peak = jnp.max(scores, axis=-1, keepdims=True)
        log_total = row_peak + jnp.log(jnp.sum(jnp.exp(scores - row_peak), axis=-1, keepdims=True))
        probs_low = jnp.exp(scores - log_total).astype(half_type)
        attended = merge_heads(
            jnp.einsum("hqk,hkd->hqd", probs_low, value_heads, preferred_element_type=float_type)
        ).astype(half_type)
        hidden = inputs_f + jnp.dot(attended, output_weight, preferred_element_type=float_type)
        routed = normalize(hidden, gain_ffn).astype(half_type)
        experts = jnp.take(hash_table, token_ids[batch])
        onehot = (experts[:, None] == jnp.arange(owners, dtype=jnp.int32)[None, :]).astype(
            jnp.int32
        )
        rank = jnp.sum((jnp.cumsum(onehot, axis=0, dtype=jnp.int32) - onehot) * onehot, axis=1)
        slot_index = experts * capacity + rank
        packed = jnp.zeros((owners * capacity, model_width), half_type).at[slot_index].set(routed)
        packed = packed.reshape(owners, capacity, model_width)
        received = lax.all_to_all(
            packed, "expert", split_axis=0, concat_axis=0, tiled=True
        ).reshape(owners * capacity, model_width)
        pre_active = jnp.dot(received, weight_in, preferred_element_type=float_type)
        active = jax.nn.silu(pre_active).astype(half_type)
        produced = jnp.dot(active, weight_out, preferred_element_type=float_type).astype(half_type)
        returned = lax.all_to_all(
            produced.reshape(owners, capacity, model_width),
            "expert",
            split_axis=0,
            concat_axis=0,
            tiled=True,
        )
        returned = returned.reshape(owners * capacity, model_width)
        block_out = hidden + jnp.take(returned, slot_index, axis=0).astype(float_type)
        outputs.append(block_out.astype(half_type))
        grad_block = cotangent[batch].astype(float_type)
        grad_result = grad_block.astype(half_type)
        grad_packed = (
            jnp.zeros((owners * capacity, model_width), half_type).at[slot_index].set(grad_result)
        )
        grad_packed = grad_packed.reshape(owners, capacity, model_width)
        grad_recv = lax.all_to_all(grad_packed, "expert", split_axis=0, concat_axis=0, tiled=True)
        grad_recv = grad_recv.reshape(owners * capacity, model_width)
        slope = smooth_slope(pre_active)
        grad_out_sum = grad_out_sum + jnp.dot(
            active.T, grad_recv, preferred_element_type=float_type
        )
        grad_active = jnp.dot(grad_recv, weight_out.T, preferred_element_type=float_type)
        grad_pre = (grad_active * slope).astype(half_type)
        grad_in_sum = grad_in_sum + jnp.dot(received.T, grad_pre, preferred_element_type=float_type)
        grad_rows = jnp.dot(grad_pre, weight_in.T, preferred_element_type=float_type).astype(
            half_type
        )
        grad_back = lax.all_to_all(
            grad_rows.reshape(owners, capacity, model_width),
            "expert",
            split_axis=0,
            concat_axis=0,
            tiled=True,
        )
        grad_routed = jnp.take(
            grad_back.reshape(owners * capacity, model_width), slot_index, axis=0
        ).astype(float_type)
        ignored_ffn, pull_ffn = jax.vjp(normalize, hidden, gain_ffn)
        grad_from_ffn, grad_gain_two = pull_ffn(grad_routed)
        grad_hidden = grad_block + grad_from_ffn
        grad_attn = grad_hidden.astype(half_type)
        grad_output_term = jnp.dot(attended.T, grad_attn, preferred_element_type=float_type)
        grad_mixed = split_heads(
            jnp.dot(grad_attn, output_weight.T, preferred_element_type=float_type).astype(
                half_type
            ),
            head_count,
        )
        scores_again = masked_scores(query_heads, key_heads, allowed, score_scale)
        probs = jnp.exp(scores_again - log_total)
        probs_again = probs.astype(half_type)
        grad_values = jnp.einsum(
            "hqk,hqd->hkd", probs_again, grad_mixed, preferred_element_type=float_type
        ).astype(half_type)
        grad_probs = jnp.einsum(
            "hqd,hkd->hqk", grad_mixed, value_heads, preferred_element_type=float_type
        )
        shared = jnp.sum(probs * grad_probs, axis=-1, keepdims=True)
        grad_scores = (probs * (grad_probs - shared)).astype(half_type)
        grad_queries = (
            jnp.einsum("hqk,hkd->hqd", grad_scores, key_heads, preferred_element_type=float_type)
            * score_scale
        ).astype(half_type)
        grad_keys = (
            jnp.einsum("hqk,hqd->hkd", grad_scores, query_heads, preferred_element_type=float_type)
            * score_scale
        ).astype(half_type)
        grad_queries = merge_heads(grad_queries)
        grad_keys = merge_heads(grad_keys)
        grad_values = merge_heads(grad_values)
        grad_query_term = jnp.dot(normed_attn.T, grad_queries, preferred_element_type=float_type)
        grad_key_term = jnp.dot(normed_attn.T, grad_keys, preferred_element_type=float_type)
        grad_value_term = jnp.dot(normed_attn.T, grad_values, preferred_element_type=float_type)
        grad_normed = (
            jnp.dot(grad_queries, query_weight.T, preferred_element_type=float_type)
            + jnp.dot(grad_keys, key_weight.T, preferred_element_type=float_type)
            + jnp.dot(grad_values, value_weight.T, preferred_element_type=float_type)
        )
        ignored_attn, pull_attn = jax.vjp(normalize, inputs_f, gain_attn)
        grad_from_attn, grad_gain_one = pull_attn(grad_normed)
        grads_in.append((grad_hidden + grad_from_attn).astype(half_type))
        terms = (
            grad_query_term,
            grad_key_term,
            grad_value_term,
            grad_output_term,
            grad_gain_one,
            grad_gain_two,
        )
        dense_total = tuple((total + term for total, term in zip(dense_total, terms)))
    dense_total = lax.psum(
        (
            dense_total[0],
            dense_total[1],
            dense_total[2],
            dense_total[3],
            dense_total[4],
            dense_total[5],
        ),
        ("dp", "expert"),
    )
    expert_in_sum, expert_out_sum = (
        lax.psum(grad_in_sum.astype(jnp.bfloat16), "dp").astype(jnp.float32),
        lax.psum(grad_out_sum.astype(jnp.bfloat16), "dp").astype(jnp.float32),
    )
    return (
        jnp.stack(outputs),
        jnp.stack(grads_in),
        dense_total[0],
        dense_total[1],
        dense_total[2],
        dense_total[3],
        dense_total[4],
        dense_total[5],
        expert_in_sum[None],
        expert_out_sum[None],
    )


def solution(mesh):
    placed = (
        P(None, ("dp", "expert"), None),
        P(None, ("dp", "expert"), None),
        P(None, ("dp", "expert")),
        P(),
        P(None, ("dp", "expert")),
        P(),
        P(),
        P(),
        P(),
        P(),
        P(),
        P("expert", None, None),
        P("expert", None, None),
    )
    return jax.shard_map(
        per_device,
        mesh=mesh,
        in_specs=placed,
        out_specs=(
            P(None, ("dp", "expert"), None),
            P(None, ("dp", "expert"), None),
            P(),
            P(),
            P(),
            P(),
            P(),
            P(),
            P("expert", None, None),
            P("expert", None, None),
        ),
        check_vma=False,
    )
```

profile of v0, /device:TPU:0, one launch (start us, length us, event | category | flops | bytes accessed | tf_op | source)
XLA Modules:
  0.0 789.7 jit_solution(1991907835853382940)
XLA Ops:
  36.2 3.9 scatter_custom_fusion
  40.1 5.7 all-to-all-start
  63.0 5.8 convolution_convert_fusion
  76.1 4.3 all-to-all-start.2
  88.1 9.2 %all-to-all-done.2 = bf16[8,96,768]{2,1,0:T(8,128)(2,1)S(1)} async-done(((bf16[8,96,768]{2,1,0:T(8,128)(2,1)}), bf16[8,96,768]{2,1,0:T(8,128)(2,1)S(1)}, u32[]{:S(2)}, u32[]{:S(2)}) %all-to-all-start.2) | async-done | bytes 1179680 | tf_op jit(solution)/shard_map/all_to_all | solution.py:111
  100.9 12.6 %multiply_convert_fusion.3 = (bf16[768,3072]{1,0:T(8,128)(2,1)}, f32[768,3072]{1,0:T(8,128)}) fusion(bf16[768,768]{1,0:T(8,128)(2,1)} %bitcast.13, bf16[1,768,3072]{2,1,0:T(8,128)(2,1)} %param.28), kind=kOutput, calls=%fused_computation.16 | convolution fusion | flops 3635675136 | bytes 20054016 | tf_op jit(solution)/shard_map/dot_general | solution.py:114
  113.5 8.5 %fusion.12 = f32[768,3072]{1,0:T(8,128)} fusion(bf16[768,768]{1,0:T(8,128)(2,1)S(1)} %bitcast.311, bf16[1,768,3072]{2,1,0:T(8,128)(2,1)} %param.28), kind=kOutput, calls=%fused_computation.40 | convolution fusion | flops 3623878656 | bytes 15335424 | tf_op jit(solution)/shard_map/dot_general | solution.py:114
  122.0 4.1 all-to-all-start.6
  126.1 8.8 %multiply_convert_fusion.1 = bf16[768,3072]{1,0:T(8,128)(2,1)S(1)} fusion(f32[768,3072]{1,0:T(8,128)} %get-tuple-element.57, bf16[768,768]{1,0:T(8,128)(2,1)S(1)} %bitcast.314, bf16[1,3072,768]{2,1,0:T(8,128)(2,1)} %param.29), kind=kOutput, calls=%fused_computation.13 | convolution fusion | flops 3645112320 | bytes 20054016 | tf_op jit(solution)/shard_map/dot_general | solution.py:139
  135.0 10.2 %fusion.145 = f32[3072,768]{1,0:T(8,128)} fusion(bf16[768,3072]{1,0:T(8,128)(2,1)} %get-tuple-element.56, bf16[768,768]{1,0:T(8,128)(2,1)S(1)} %bitcast.315), kind=kOutput, calls=%fused_computation.230 | convolution fusion | flops 3623878656 | bytes 15335424 | tf_op jit(solution)/shard_map/dot_general | solution.py:136
  145.2 7.2 fusion.20
  152.4 4.4 all-to-all-start.5
  156.9 8.9 %multiply_convert_fusion = bf16[768,3072]{1,0:T(8,128)(2,1)S(1)} fusion(f32[768,3072]{1,0:T(8,128)} %fusion.12, bf16[768,768]{1,0:T(8,128)(2,1)S(1)} %bitcast.316, bf16[1,3072,768]{2,1,0:T(8,128)(2,1)} %param.29), kind=kOutput, calls=%fused_computation.12 | convolution fusion | flops 3645112320 | bytes 20054016 | tf_op jit(solution)/shard_map/dot_general | solution.py:139
  165.8 15.0 %fusion.17 = bf16[1,3072,768]{2,1,0:T(8,128)(2,1)} fusion(f32[3072,768]{1,0:T(8,128)} %fusion.145, bf16[768,768]{1,0:T(8,128)(2,1)S(1)} %bitcast.317, f32[768,3072]{1,0:T(8,128)} %fusion.12), kind=kOutput, calls=%fused_computation.45 | convolution fusion | flops 3640393728 | bytes 24772608 | tf_op jit(solution)/shard_map/dot_general | solution.py:136
  180.9 4.9 fusion.23
  185.7 4.6 all-to-all-start.7
  190.4 11.1 %fusion.29 = bf16[768,768]{1,0:T(8,128)(2,1)} fusion(bf16[1,3072,768]{2,1,0:T(8,128)(2,1)} %param.29, f32[768,3072]{1,0:T(8,128)} %fusion.12), kind=kOutput, calls=%fused_computation.59 | convolution fusion | flops 3636264960 | bytes 15335424 | tf_op jit(solution)/shard_map/dot_general | solution.py:116
  201.4 5.7 all-to-all-done.7
  207.2 4.3 all-to-all-start.3
  211.4 10.3 %fusion.144 = f32[768,3072]{1,0:T(8,128)} fusion(bf16[768,768]{1,0:T(8,128)(2,1)} %bitcast.13, bf16[768,3072]{1,0:T(8,128)(2,1)} %copy-done.26), kind=kOutput, calls=%fused_computation.229 | convolution fusion | flops 3623878656 | bytes 15335424 | tf_op jit(solution)/shard_map/dot_general | solution.py:141
  221.8 8.6 %fusion.26 = bf16[768,768]{1,0:T(8,128)(2,1)} fusion(bf16[768,3072]{1,0:T(8,128)(2,1)} %get-tuple-element.56, bf16[1,3072,768]{2,1,0:T(8,128)(2,1)} %param.29), kind=kOutput, calls=%fused_computation.58 | convolution fusion | flops 3624468480 | bytes 10616832 | tf_op jit(solution)/shard_map/dot_general | solution.py:116
  230.4 4.3 all-to-all-start.1
  234.9 11.5 %fusion.16 = bf16[1,768,3072]{2,1,0:T(8,128)(2,1)} fusion(f32[768,3072]{1,0:T(8,128)} %fusion.144, bf16[768,768]{1,0:T(8,128)(2,1)} %bitcast.312, bf16[768,3072]{1,0:T(8,128)(2,1)} %copy-done.92), kind=kOutput, calls=%fused_computation.44 | convolution fusion | flops 3628597248 | bytes 20054016 | tf_op jit(solution)/shard_map/dot_general | solution.py:141
  249.7 4.4 gather_fusion.3
  260.6 4.4 gather_fusion.1
  265.0 4.2 fusion.70
  277.9 5.6 multiply_reduce_fusion.1
  325.5 46.7 %all-reduce = (f32[768]{0:T(1024)}, f32[768]{0:T(1024)}) all-reduce(f32[768]{0:T(1024)} %add.207, f32[768]{0:T(1024)} %add.208), channel_id=1, replica_groups=mesh['dp'=4,'expert'=8] {'dp','expert'}, use_global_device_ids=true, to_apply=%region_30.33 | all-reduce | flops 1536 | bytes 12288 | tf_op jit(solution)/shard_map/psum | solution.py:208
  378.5 196.6 %all-reduce.8.cloned.1.call-done = (bf16[1,768,3072]{2,1,0:T(8,128)(2,1)}, bf16[1,3072,768]{2,1,0:T(8,128)(2,1)}) async-done(((bf16[1,768,3072]{2,1,0:T(8,128)(2,1)}, bf16[1,3072,768]{2,1,0:T(8,128)(2,1)}), (bf16[1,768,3072]{2,1,0:T(8,128)(2,1)}, bf16[1,3072,768]{2,1,0:T(8,128)(2,1)})) %all-reduce.8.cloned.1.call-update) | async-done | bytes 9437200 | tf_op jit(solution)/shard_map/psum | solution.py:220
  575.1 7.5 broadcast_in_dim.117
  582.6 4.9 broadcast_in_dim.119
  587.5 185.4 %all-reduce.6.cloned.1.call-done = (f32[768,768]{1,0:T(8,128)}, f32[768,768]{1,0:T(8,128)}, f32[768,768]{1,0:T(8,128)}, f32[768,768]{1,0:T(8,128)}) async-done(((f32[768,768]{1,0:T(8,128)}, f32[768,768]{1,0:T(8,128)}, f32[768,768]{1,0:T(8,128)}, f32[768,768]{1,0:T(8,128)}), (f32[768,768]{1,0:T(8,128)}, f32[768,768]{1,0:T(8,128)}, f32[768,768]{1,0:T(8,128)}, ...) | async-done | bytes 9437200 | tf_op jit(solution)/shard_map/psum | solution.py:208
  (309 shorter events, 140.4 us)
Async XLA Ops:
  8.9 36.9 %copy-start.79 = (f32[384]{0:T(512)}, f32[384]{0:T(512)S(1)}, u32[]{:S(2)}) copy-start(f32[384]{0:T(512)S(1)} %get-tuple-element.23) | copy-start | bytes 4612
  9.5 8.2 %copy-start.69 = (f32[384]{0:T(512)}, f32[384]{0:T(512)S(1)}, u32[]{:S(2)}) copy-start(f32[384]{0:T(512)S(1)} %fusion.115) | copy-start | bytes 4612
  17.7 4.4 copy-start.11
  31.1 5.1 copy-start.67
  31.7 8.4 %copy-start.73 = (f32[384]{0:T(512)}, f32[384]{0:T(512)S(1)}, u32[]{:S(2)}) copy-start(f32[384]{0:T(512)S(1)} %fusion.116) | copy-start | bytes 4612
  40.1 36.0 %all-to-all-start = ((bf16[8,96,768]{2,1,0:T(8,128)(2,1)}), bf16[8,96,768]{2,1,0:T(8,128)(2,1)}, u32[]{:S(2)}, u32[]{:S(2)}) async-start(bf16[8,96,768]{2,1,0:T(8,128)(2,1)} %bitcast.300), calls=%async_computation | async-start | bytes 2359296 | tf_op jit(solution)/shard_map/all_to_all | solution.py:111
  51.3 11.7 %copy-start.40 = (pred[384,384]{0,1:T(8,128)(4,1)}, pred[384,384]{0,1:T(8,128)(4,1)S(1)}, u32[]{:S(2)}) copy-start(pred[384,384]{0,1:T(8,128)(4,1)S(1)} %fusion.96) | copy-start | bytes 442372
  52.8 4.7 copy-start.15
  60.4 8.4 %copy-start.63 = (f32[12,384]{1,0:T(8,128)}, f32[12,384]{1,0:T(8,128)S(1)}, u32[]{:S(2)}) copy-start(f32[12,384]{1,0:T(8,128)S(1)} %log_add_fusion) | copy-start | bytes 55300
  76.1 4.4 copy-start.27
  76.1 21.2 %all-to-all-start.2 = ((bf16[8,96,768]{2,1,0:T(8,128)(2,1)}), bf16[8,96,768]{2,1,0:T(8,128)(2,1)S(1)}, u32[]{:S(2)}, u32[]{:S(2)}) async-start(bf16[8,96,768]{2,1,0:T(8,128)(2,1)} %bitcast.31), calls=%async_computation.2 | async-start | bytes 2359296 | tf_op jit(solution)/shard_map/all_to_all | solution.py:111
  97.3 16.2 %copy-start.54 = (bf16[8,96,768]{2,1,0:T(8,128)(2,1)}, bf16[8,96,768]{2,1,0:T(8,128)(2,1)S(1)}, u32[]{:S(2)}) copy-start(bf16[8,96,768]{2,1,0:T(8,128)(2,1)S(1)} %all-to-all-done.2) | copy-start | bytes 3538948
  97.3 24.7 %all-to-all-start.4 = ((bf16[8,96,768]{2,1,0:T(8,128)(2,1)}), bf16[8,96,768]{2,1,0:T(8,128)(2,1)S(1)}, u32[]{:S(2)}, u32[]{:S(2)}) async-start(bf16[8,96,768]{2,1,0:T(8,128)(2,1)} %bitcast.37), calls=%async_computation.4 | async-start | bytes 2359296 | tf_op jit(solution)/shard_map/all_to_all | solution.py:133
  122.0 30.4 %all-to-all-start.6 = ((bf16[8,96,768]{2,1,0:T(8,128)(2,1)}), bf16[8,96,768]{2,1,0:T(8,128)(2,1)S(1)}, u32[]{:S(2)}, u32[]{:S(2)}) async-start(bf16[8,96,768]{2,1,0:T(8,128)(2,1)} %bitcast.55), calls=%async_computation.6 | async-start | bytes 2359296 | tf_op jit(solution)/shard_map/all_to_all | solution.py:133
  134.9 10.3 %copy-start.26 = (bf16[768,3072]{1,0:T(8,128)(2,1)}, bf16[768,3072]{1,0:T(8,128)(2,1)S(1)}, u32[]{:S(2)}) copy-start(bf16[768,3072]{1,0:T(8,128)(2,1)S(1)} %multiply_convert_fusion.1) | copy-start | bytes 14155780
  152.4 33.3 %all-to-all-start.5 = ((bf16[8,96,768]{2,1,0:T(8,128)(2,1)}), bf16[8,96,768]{2,1,0:T(8,128)(2,1)S(1)}, u32[]{:S(2)}, u32[]{:S(2)}) async-start(bf16[8,96,768]{2,1,0:T(8,128)(2,1)} %bitcast.319), calls=%async_computation.5 | async-start | bytes 2359296 | tf_op jit(solution)/shard_map/all_to_all | solution.py:145
  156.8 24.0 %slice-start.4 = ((s8[4718592]{0:T(1024)(128)(4,1)}), s8[4194304]{0:T(1024)(128)(4,1)S(1)}, s32[]{:S(2)}) async-start(s8[4718592]{0:T(1024)(128)(4,1)} %bitcast.331), calls=%async_computation.14 | async-start | bytes 8388608
  165.8 15.0 %copy-start.92 = (bf16[768,3072]{1,0:T(8,128)(2,1)}, bf16[768,3072]{1,0:T(8,128)(2,1)S(1)}, u32[]{:S(2)}) copy-start(bf16[768,3072]{1,0:T(8,128)(2,1)S(1)} %multiply_convert_fusion) | copy-start | bytes 14155780
  165.8 15.0 %slice-start.5 = ((s8[4718592]{0:T(1024)(128)(4,1)}), s8[524288]{0:T(1024)(128)(4,1)S(1)}, s32[]{:S(2)}) async-start(s8[4718592]{0:T(1024)(128)(4,1)} %bitcast.331), calls=%async_computation.15 | async-start | bytes 1048576
  185.7 21.4 %all-to-all-start.7 = ((bf16[8,96,768]{2,1,0:T(8,128)(2,1)}), bf16[8,96,768]{2,1,0:T(8,128)(2,1)S(1)}, u32[]{:S(2)}, u32[]{:S(2)}) async-start(bf16[8,96,768]{2,1,0:T(8,128)(2,1)} %bitcast.320), calls=%async_computation.7 | async-start | bytes 2359296 | tf_op jit(solution)/shard_map/all_to_all | solution.py:145
  207.2 23.2 %all-to-all-start.3 = ((bf16[8,96,768]{2,1,0:T(8,128)(2,1)}), bf16[8,96,768]{2,1,0:T(8,128)(2,1)}, u32[]{:S(2)}, u32[]{:S(2)}) async-start(bf16[8,96,768]{2,1,0:T(8,128)(2,1)} %bitcast.318), calls=%async_computation.3 | async-start | bytes 2359296 | tf_op jit(solution)/shard_map/all_to_all | solution.py:117
  230.4 30.2 %all-to-all-start.1 = ((bf16[8,96,768]{2,1,0:T(8,128)(2,1)}), bf16[8,96,768]{2,1,0:T(8,128)(2,1)}, u32[]{:S(2)}, u32[]{:S(2)}) async-start(bf16[8,96,768]{2,1,0:T(8,128)(2,1)} %bitcast.313), calls=%async_computation.1 | async-start | bytes 2359296 | tf_op jit(solution)/shard_map/all_to_all | solution.py:117
  234.6 340.4 %all-reduce.8.cloned.1.call-start = ((), (), s32[]{:S(2)}) async-start(), calls=%async_computation.9 | async-start | bytes 18874368 | tf_op jit(solution)/shard_map/psum | solution.py:220
  246.4 526.4 %all-reduce.6.cloned.1.call-start = ((), (), s32[]{:S(2)}) async-start(), calls=%async_computation.8 | async-start | bytes 18874368 | tf_op jit(solution)/shard_map/psum | solution.py:208
  249.7 4.5 copy-start.81
  260.6 4.4 copy-start.88
  277.9 5.7 slice-start
  277.9 5.7 slice-start.1
  288.2 7.2 slice-start.2
  291.0 4.5 slice-start.3
  321.8 53.0 %copy-start.80 = (f32[384]{0:T(512)S(1)}, f32[384]{0:T(512)}, u32[]{:S(2)}) copy-start(f32[384]{0:T(512)} %copy-done.79) | copy-start | bytes 4612
  575.1 7.5 copy-start.25
  (77 other events, 164.5 us)
Sparse Core Ops, SparseCore 0:
  246.5 328.4 all-reduce.7
  581.9 190.9 all-reduce.5
where the time goes:
time: 799 us; the launch traced here: 790 us
  waiting for transfers between devices  397 us (50%)
  matrix products  184 us (23%)
  local copies, waits for them, and re-layouts  61.3 us (8%)
  other arithmetic  49.6 us (6%)
  blocking collectives  46.7 us (6%)
  starting transfers between devices  35.6 us (4%)
  between operations  15.4 us (2%)
    psum x1, waiting for transfers between devices, per_device(): lax.psum(grad_in_sum.astype(jnp.bfloat16), 'dp').astype(jnp.float32)  197 us
    psum x1, waiting for transfers between devices, per_device(): lax.psum((dense_total[0], dense_total[1], dense_total[2], dense_total[3],...  185 us
    psum x1, blocking collectives, per_device(): lax.psum((dense_total[0], dense_total[1], dense_total[2], dense_total[3],...  46.7 us
    dot_general x2, matrix products, per_device(): jnp.dot(active.T, grad_recv, preferred_element_type=float_type)  25.3 us
    dot_general x2, matrix products, per_device(): jnp.dot(received.T, grad_pre, preferred_element_type=float_type)  21.9 us
    dot_general x2, matrix products, per_device(): pre_active = jnp.dot(received, weight_in, preferred_element_type=float_type)  21.1 us
    unnamed x202, local copies, waits for them, and re-layouts  20.3 us
    dot_general x2, matrix products, per_device(): jnp.dot(active, weight_out, preferred_element_type=float_type)  19.7 us
  transfers between devices with their start and end apart: 10, of which 4 were waited for; matrix products, arithmetic and copies ran while one was open for 31% of the time, Pallas kernels for 0%

commit v1 on v0

--- a/solution.py
+++ b/solution.py
@@ -217,7 +217,7 @@
         ("dp", "expert"),
     )
     expert_in_sum, expert_out_sum = (
-        lax.psum(grad_in_sum.astype(jnp.bfloat16), "dp").astype(jnp.float32),
+        jnp.sum(lax.all_gather(grad_in_sum.astype(jnp.bfloat16), "dp"), axis=0).astype(jnp.float32),
         lax.psum(grad_out_sum.astype(jnp.bfloat16), "dp").astype(jnp.float32),
     )
     return (

time: 799 us -> 870 us (1.089)
  waiting for transfers between devices: 397 us -> 458 us
  other arithmetic: 49.6 us -> 62.2 us
  matrix products: 184 us -> 174 us
    all_gather x0 -> x1, waiting for transfers between devices: none -> 241 us  [per_device(): lax.all_gather(grad_in_sum.astype(jnp.bfloat16), 'dp')]
    psum x1, waiting for transfers between devices: 197 us -> 0.01 us  [per_device(): lax.psum(grad_out_sum.astype(jnp.bfloat16), 'dp').astype(jnp.float32)]
    all_to_all x2, waiting for transfers between devices: 0.01 us -> 15.1 us  [per_device(): lax.all_to_all(produced.reshape(owners, capacity, model_width), 'expert',...]
    reduce_sum x0 -> x1, other arithmetic: none -> 13.7 us  [per_device(): jnp.sum(lax.all_gather(grad_in_sum.astype(jnp.bfloat16), 'dp'), axis=0)]
    dot_general x2, matrix products: 21.9 us -> 12 us  [per_device(): jnp.dot(received.T, grad_pre, preferred_element_type=float_type)]
    psum x1, waiting for transfers between devices: 185 us -> 177 us  [per_device(): lax.psum((dense_total[0], dense_total[1], dense_total[2], dense_total[3],...]
    unnamed x202 -> x212, local copies, waits for them, and re-layouts: 20.3 us -> 23 us
  transfers between devices with their start and end apart: 10 -> 11, of which waited for: 4 -> 9; matrix products, arithmetic and copies ran while one was open for 31% -> 27% of each run, Pallas kernels for 0% -> 0%
where the time goes in v1:
time: 870 us; the launch traced here: 860 us
  waiting for transfers between devices  458 us (53%)
  matrix products  174 us (20%)
  local copies, waits for them, and re-layouts  65 us (7%)
  other arithmetic  62.2 us (7%)
  blocking collectives  51.3 us (6%)
  starting transfers between devices  34.4 us (4%)
  between operations  15.2 us (2%)
    all_gather x1, waiting for transfers between devices, per_device(): lax.all_gather(grad_in_sum.astype(jnp.bfloat16), 'dp')  241 us
    psum x1, waiting for transfers between devices, per_device(): lax.psum((dense_total[0], dense_total[1], dense_total[2], dense_total[3],...  177 us
    psum x1, blocking collectives, per_device(): lax.psum((dense_total[0], dense_total[1], dense_total[2], dense_total[3],...  51.3 us
    unnamed x212, local copies, waits for them, and re-layouts  23 us
    dot_general x2, matrix products, per_device(): pre_active = jnp.dot(received, weight_in, preferred_element_type=float_type)  21.3 us
    dot_general x2, matrix products, per_device(): jnp.dot(active.T, grad_recv, preferred_element_type=float_type)  21 us
    dot_general x2, matrix products, per_device(): jnp.dot(active, weight_out, preferred_element_type=float_type)  19.9 us
    dot_general x2, matrix products, per_device(): jnp.dot(grad_recv, weight_out.T, preferred_element_type=float_type)  17.7 us
  transfers between devices with their start and end apart: 11, of which 9 were waited for; matrix products, arithmetic and copies ran while one was open for 27% of the time, Pallas kernels for 0%

profile of v1, /device:TPU:0, one launch (start us, length us, event | category | flops | bytes accessed | tf_op | source)
XLA Modules:
  0.0 860.1 jit_solution(10636420905598548032)
XLA Ops:
  40.2 5.5 all-to-all-start
  71.8 4.9 all-to-all-start.4
  76.8 5.0 convolution_convert_fusion
  86.5 7.2 all-to-all-done.4
  97.2 12.6 %multiply_convert_fusion.3 = (bf16[768,3072]{1,0:T(8,128)(2,1)}, f32[768,3072]{1,0:T(8,128)}) fusion(bf16[768,768]{1,0:T(8,128)(2,1)} %bitcast.13, bf16[1,768,3072]{2,1,0:T(8,128)(2,1)} %param.28), kind=kOutput, calls=%fused_computation.16 | convolution fusion | flops 3635675136 | bytes 20054016 | tf_op jit(solution)/shard_map/dot_general | solution.py:114
  109.8 4.2 all-to-all-done.2
  117.8 8.7 %fusion.12 = f32[768,3072]{1,0:T(8,128)} fusion(bf16[768,768]{1,0:T(8,128)(2,1)S(1)} %bitcast.314, bf16[1,768,3072]{2,1,0:T(8,128)(2,1)} %param.28), kind=kOutput, calls=%fused_computation.41 | convolution fusion | flops 3623878656 | bytes 15335424 | tf_op jit(solution)/shard_map/dot_general | solution.py:114
  126.5 7.6 fusion.144
  134.3 13.4 %fusion.16 = bf16[1,3072,768]{2,1,0:T(8,128)(2,1)} fusion(f32[3072,768]{1,0:T(8,128)} %fusion.144, bf16[768,768]{1,0:T(8,128)(2,1)S(1)} %bitcast.316, f32[768,3072]{1,0:T(8,128)} %fusion.12), kind=kOutput, calls=%fused_computation.45 | convolution fusion | flops 3640393728 | bytes 24772608 | tf_op jit(solution)/shard_map/dot_general | solution.py:136
  147.9 8.9 %multiply_convert_fusion.1 = bf16[768,3072]{1,0:T(8,128)(2,1)S(1)} fusion(f32[768,3072]{1,0:T(8,128)} %get-tuple-element.55, bf16[768,768]{1,0:T(8,128)(2,1)} %bitcast.38, bf16[1,3072,768]{2,1,0:T(8,128)(2,1)} %param.29), kind=kOutput, calls=%fused_computation.13 | convolution fusion | flops 3645112320 | bytes 20054016 | tf_op jit(solution)/shard_map/dot_general | solution.py:139
  156.8 6.0 fusion.143
  162.9 8.9 %multiply_convert_fusion = bf16[768,3072]{1,0:T(8,128)(2,1)S(1)} fusion(f32[768,3072]{1,0:T(8,128)} %fusion.12, bf16[768,768]{1,0:T(8,128)(2,1)S(1)} %bitcast.317, bf16[1,3072,768]{2,1,0:T(8,128)(2,1)} %param.29), kind=kOutput, calls=%fused_computation.12 | convolution fusion | flops 3645112320 | bytes 20054016 | tf_op jit(solution)/shard_map/dot_general | solution.py:139
  173.9 6.0 add_convert_fusion.1
  179.9 8.6 %fusion.19 = bf16[768,768]{1,0:T(8,128)(2,1)} fusion(bf16[768,3072]{1,0:T(8,128)(2,1)} %copy-done.30, bf16[1,768,3072]{2,1,0:T(8,128)(2,1)} %param.28), kind=kOutput, calls=%fused_computation.56 | convolution fusion | flops 3624468480 | bytes 10616832 | tf_op jit(solution)/shard_map/dot_general | solution.py:142
  192.4 8.8 %fusion.22 = bf16[768,768]{1,0:T(8,128)(2,1)} fusion(bf16[768,3072]{1,0:T(8,128)(2,1)} %copy-done.98, bf16[1,768,3072]{2,1,0:T(8,128)(2,1)} %param.28), kind=kOutput, calls=%fused_computation.57 | convolution fusion | flops 3624468480 | bytes 10616832 | tf_op jit(solution)/shard_map/dot_general | solution.py:142
  201.2 8.1 all-to-all-done.5
  212.8 11.2 %fusion.28 = bf16[768,768]{1,0:T(8,128)(2,1)} fusion(bf16[1,3072,768]{2,1,0:T(8,128)(2,1)} %param.29, f32[768,3072]{1,0:T(8,128)} %fusion.12), kind=kOutput, calls=%fused_computation.59 | convolution fusion | flops 3636264960 | bytes 15335424 | tf_op jit(solution)/shard_map/dot_general | solution.py:116
  224.0 5.6 all-to-all-done.7
  229.6 4.4 all-to-all-start.3
  234.0 8.7 %fusion.25 = bf16[768,768]{1,0:T(8,128)(2,1)} fusion(bf16[768,3072]{1,0:T(8,128)(2,1)} %get-tuple-element.54, bf16[1,3072,768]{2,1,0:T(8,128)(2,1)} %param.29), kind=kOutput, calls=%fused_computation.58 | convolution fusion | flops 3624468480 | bytes 10616832 | tf_op jit(solution)/shard_map/dot_general | solution.py:116
  242.7 8.1 all-to-all-done.3
  250.8 4.4 all-to-all-start.1
  258.0 4.4 gather_fusion.3
  265.1 7.0 all-to-all-done.1
  272.1 4.6 gather_fusion.1
  291.8 5.7 multiply_reduce_fusion.1
  340.4 51.3 %all-reduce = (f32[768]{0:T(1024)}, f32[768]{0:T(1024)}) all-reduce(f32[768]{0:T(1024)} %add.205, f32[768]{0:T(1024)} %add.206), channel_id=1, replica_groups=mesh['dp'=4,'expert'=8] {'dp','expert'}, use_global_device_ids=true, to_apply=%region_30.33 | all-reduce | flops 1536 | bytes 12288 | tf_op jit(solution)/shard_map/psum | solution.py:208
  397.9 6.9 broadcast_in_dim.112
  404.8 241.1 %all-gather.3.cloned.1.call-done = bf16[3072,3072]{1,0:T(8,128)(2,1)} async-done(((bf16[768,3072]{1,0:T(8,128)(2,1)}), bf16[3072,3072]{1,0:T(8,128)(2,1)}) %all-gather.3.cloned.1.call-update) | async-done | bytes 18874384 | tf_op jit(solution)/shard_map/all_gather | solution.py:220
  645.9 13.7 %reduce_sum.203 = bf16[768,3072]{1,0:T(8,128)(2,1)} reduce(bf16[4,768,3072]{2,1,0:T(8,128)(2,1)} %bitcast.286, bf16[]{:T(256)} %constant.58.clone.1), dimensions={0}, to_apply=%region_34.37 | reduce | flops 7077888 | bytes 23592962 | tf_op jit(solution)/shard_map/reduce_sum | solution.py:220
  659.6 7.4 bitcast_convert_fusion
  667.0 176.5 %all-reduce.7.cloned.1.call-done = (f32[768,768]{1,0:T(8,128)}, f32[768,768]{1,0:T(8,128)}, f32[768,768]{1,0:T(8,128)}, f32[768,768]{1,0:T(8,128)}) async-done(((f32[768,768]{1,0:T(8,128)}, f32[768,768]{1,0:T(8,128)}, f32[768,768]{1,0:T(8,128)}, f32[768,768]{1,0:T(8,128)}), (f32[768,768]{1,0:T(8,128)}, f32[768,768]{1,0:T(8,128)}, f32[768,768]{1,0:T(8,128)}, ...) | async-done | bytes 9437200 | tf_op jit(solution)/shard_map/psum | solution.py:208
  (322 shorter events, 159.6 us)
Async XLA Ops:
  8.9 36.8 %copy-start.83 = (f32[384]{0:T(512)}, f32[384]{0:T(512)S(1)}, u32[]{:S(2)}) copy-start(f32[384]{0:T(512)S(1)} %get-tuple-element.23) | copy-start | bytes 4612
  9.5 8.2 copy-start.73
  31.2 5.0 copy-start.71
  31.8 8.4 copy-start.77
  36.3 13.8 %copy-start.89 = (s32[384]{0:T(512)}, s32[384]{0:T(512)S(1)}, u32[]{:S(2)}) copy-start(s32[384]{0:T(512)S(1)} %get-tuple-element.35) | copy-start | bytes 4612
  40.2 31.6 %all-to-all-start = ((bf16[8,96,768]{2,1,0:T(8,128)(2,1)}), bf16[8,96,768]{2,1,0:T(8,128)(2,1)}, u32[]{:S(2)}, u32[]{:S(2)}) async-start(bf16[8,96,768]{2,1,0:T(8,128)(2,1)} %bitcast.303), calls=%async_computation | async-start | bytes 2359296 | tf_op jit(solution)/shard_map/all_to_all | solution.py:111
  54.9 21.9 %copy-start.44 = (pred[384,384]{0,1:T(8,128)(4,1)}, pred[384,384]{0,1:T(8,128)(4,1)S(1)}, u32[]{:S(2)}) copy-start(pred[384,384]{0,1:T(8,128)(4,1)S(1)} %fusion.95) | copy-start | bytes 442372
  56.3 10.3 %copy-start.18 = (bf16[384,768]{0,1:T(8,128)(2,1)}, bf16[384,768]{0,1:T(8,128)(2,1)S(1)}, u32[]{:S(2)}) copy-start(bf16[384,768]{0,1:T(8,128)(2,1)S(1)} %copy.43) | copy-start | bytes 1769476
  63.0 20.2 %copy-start.93 = (s32[384]{0:T(512)}, s32[384]{0:T(512)S(1)}, u32[]{:S(2)}) copy-start(s32[384]{0:T(512)S(1)} %get-tuple-element.37) | copy-start | bytes 4612
  71.8 5.0 copy-start.67
  71.8 5.0 copy-start.53
  71.8 21.8 %all-to-all-start.4 = ((bf16[8,96,768]{2,1,0:T(8,128)(2,1)}), bf16[8,96,768]{2,1,0:T(8,128)(2,1)}, u32[]{:S(2)}, u32[]{:S(2)}) async-start(bf16[8,96,768]{2,1,0:T(8,128)(2,1)} %bitcast.37), calls=%async_computation.4 | async-start | bytes 2359296 | tf_op jit(solution)/shard_map/all_to_all | solution.py:133
  76.8 5.0 copy-start.32
  93.6 20.3 %all-to-all-start.2 = ((bf16[8,96,768]{2,1,0:T(8,128)(2,1)}), bf16[8,96,768]{2,1,0:T(8,128)(2,1)S(1)}, u32[]{:S(2)}, u32[]{:S(2)}) async-start(bf16[8,96,768]{2,1,0:T(8,128)(2,1)} %bitcast.31), calls=%async_computation.2 | async-start | bytes 2359296 | tf_op jit(solution)/shard_map/all_to_all | solution.py:111
  114.0 20.3 %all-to-all-start.6 = ((bf16[8,96,768]{2,1,0:T(8,128)(2,1)}), bf16[8,96,768]{2,1,0:T(8,128)(2,1)S(1)}, u32[]{:S(2)}, u32[]{:S(2)}) async-start(bf16[8,96,768]{2,1,0:T(8,128)(2,1)} %bitcast.55), calls=%async_computation.6 | async-start | bytes 2359296 | tf_op jit(solution)/shard_map/all_to_all | solution.py:133
  117.5 280.4 %all-reduce.5.cloned.1.call-start = ((), (), s32[]{:S(2)}) async-start(), calls=%async_computation.8 | async-start | bytes 9437184 | tf_op jit(solution)/shard_map/psum | solution.py:221
  117.7 8.7 %copy-start.99 = (bf16[768,3072]{1,0:T(8,128)(2,1)S(1)}, bf16[768,3072]{1,0:T(8,128)(2,1)}, u32[]{:S(2)}) copy-start(bf16[768,3072]{1,0:T(8,128)(2,1)} %get-tuple-element.54) | copy-start | bytes 14155780
  147.7 498.2 %all-gather.3.cloned.1.call-start = ((), (), s32[]{:S(2)}) async-start(), calls=%async_computation.9 | async-start | bytes 23592960 | tf_op jit(solution)/shard_map/all_gather | solution.py:220
  156.8 6.0 copy-start.30
  188.5 20.7 %all-to-all-start.5 = ((bf16[8,96,768]{2,1,0:T(8,128)(2,1)}), bf16[8,96,768]{2,1,0:T(8,128)(2,1)S(1)}, u32[]{:S(2)}, u32[]{:S(2)}) async-start(bf16[8,96,768]{2,1,0:T(8,128)(2,1)} %bitcast.39), calls=%async_computation.5 | async-start | bytes 2359296 | tf_op jit(solution)/shard_map/all_to_all | solution.py:145
  209.3 20.3 %all-to-all-start.7 = ((bf16[8,96,768]{2,1,0:T(8,128)(2,1)}), bf16[8,96,768]{2,1,0:T(8,128)(2,1)S(1)}, u32[]{:S(2)}, u32[]{:S(2)}) async-start(bf16[8,96,768]{2,1,0:T(8,128)(2,1)} %bitcast.319), calls=%async_computation.7 | async-start | bytes 2359296 | tf_op jit(solution)/shard_map/all_to_all | solution.py:145
  229.6 21.3 %all-to-all-start.3 = ((bf16[8,96,768]{2,1,0:T(8,128)(2,1)}), bf16[8,96,768]{2,1,0:T(8,128)(2,1)}, u32[]{:S(2)}, u32[]{:S(2)}) async-start(bf16[8,96,768]{2,1,0:T(8,128)(2,1)} %bitcast.320), calls=%async_computation.3 | async-start | bytes 2359296 | tf_op jit(solution)/shard_map/all_to_all | solution.py:117
  250.8 21.2 %all-to-all-start.1 = ((bf16[8,96,768]{2,1,0:T(8,128)(2,1)}), bf16[8,96,768]{2,1,0:T(8,128)(2,1)}, u32[]{:S(2)}, u32[]{:S(2)}) async-start(bf16[8,96,768]{2,1,0:T(8,128)(2,1)} %bitcast.318), calls=%async_computation.1 | async-start | bytes 2359296 | tf_op jit(solution)/shard_map/all_to_all | solution.py:117
  255.2 588.3 %all-reduce.7.cloned.1.call-start = ((), (), s32[]{:S(2)}) async-start(), calls=%async_computation.10 | async-start | bytes 18874368 | tf_op jit(solution)/shard_map/psum | solution.py:208
  272.1 4.6 copy-start.12
  272.1 4.6 copy-start.72
  272.1 4.6 copy-start.78
  272.1 4.6 copy-start.80
  291.8 5.7 slice-start
  291.8 5.7 slice-start.1
  302.1 7.2 slice-start.2
  336.6 57.6 %copy-start.84 = (f32[384]{0:T(512)S(1)}, f32[384]{0:T(512)}, u32[]{:S(2)}) copy-start(f32[384]{0:T(512)} %copy-done.83) | copy-start | bytes 4612
  (83 other events, 187.8 us)
Sparse Core Ops, SparseCore 0:
  147.8 173.7 all-reduce.4
  323.2 322.6 all-gather.2
  652.7 190.7 all-reduce.6
